TPU v7x, 32 devices: a whole 2x2x4 slice. The times are simulated.
32 devices in a mesh: gx: 4 (over y, x), gy: 2 (over core), gz: 4 (over z).
Axes of the slice: x: 2, y: 2, z: 4, core: 2. Of those that a mesh axis runs over, the one named last changes fastest.
Arguments:
- pair: bfloat16 [128, 1024, 1024], P('gz', 'gy', 'gx'), may hold values from -6 to 6
- pair_mask: int32 [1024, 1024], P('gy', 'gx'), may hold values 0 or 1
- in_gain: float32 [128], replicated, may hold values from 0.5 to 2
- w_left: bfloat16 [128, 128], P(None, 'gz'), may hold values from -0.5 to 0.5
- w_left_gate: bfloat16 [128, 128], P(None, 'gz'), may hold values from -0.5 to 0.5
- w_right: bfloat16 [128, 128], P(None, 'gz'), may hold values from -0.5 to 0.5
- w_right_gate: bfloat16 [128, 128], P(None, 'gz'), may hold values from -0.5 to 0.5
- w_out_gate: bfloat16 [128, 128], P(None, 'gz'), may hold values from -0.5 to 0.5
- out_gain: float32 [128], P('gz'), may hold values from 0.5 to 2
- w_out: bfloat16 [128, 128], P(None, 'gz'), may hold values from -0.5 to 0.5
Outputs:
- update: bfloat16 [128, 1024, 1024], P('gz', 'gy', 'gx')
All inputs are finite; a program needn't handle non-finite values. No bound on the sum of `pair_mask` on one device may be relied on, other than what follows from the above.
Results may differ from a plain program's by a relative error of at most 0.0078.
Values may be sent and summed in bfloat16 or wider, within the bound.
No kernel may reach another device: no remote copies, remote signals or barrier semaphores. Data moves between devices by JAX's collectives and lax.ppermute only.
A program may use at most 192 MiB of HBM per device.

v0:
```python
import jax
import jax.numpy as jnp
from jax import lax
from jax.sharding import PartitionSpec as P

epsilon = 1e-05


def local(
    pair,
    pair_mask,
    in_gain,
    w_left,
    w_left_gate,
    w_right,
    w_right_gate,
    w_out_gate,
    out_gain,
    w_out,
):
    gathered = lax.all_gather(pair, "gz", axis=0, tiled=True).astype(jnp.float32)
    average = jnp.mean(gathered, axis=0)
    centered = gathered - average
    spread = jnp.mean(jnp.square(centered), axis=0)
    normed = (centered * lax.rsqrt(spread + epsilon) * in_gain[:, None, None]).astype(jnp.bfloat16)
    mask_float = pair_mask.astype(jnp.float32)[None]

    def project(weight):
        return jnp.einsum("cik,ch->hik", normed, weight, preferred_element_type=jnp.float32)

    left_rows = (mask_float * jax.nn.sigmoid(project(w_left_gate)) * project(w_left)).astype(
        jnp.bfloat16
    )
    right_rows = (mask_float * jax.nn.sigmoid(project(w_right_gate)) * project(w_right)).astype(
        jnp.bfloat16
    )
    out_gate = jax.nn.sigmoid(
        jnp.einsum("cij,cd->dij", normed, w_out_gate, preferred_element_type=jnp.float32)
    )
    left_group, right_group = (
        lax.all_to_all(left_rows, "gx", split_axis=0, concat_axis=2, tiled=True),
        lax.all_to_all(right_rows, "gx", split_axis=0, concat_axis=2, tiled=True),
    )
    full_product = lax.dot_general(
        left_group,
        lax.all_gather(right_group, "gy", axis=1, tiled=True),
        (((2,), (2,)), ((0,), (0,))),
        preferred_element_type=jnp.float32,
    )
    mixed_sum = lax.all_to_all(full_product, "gx", split_axis=2, concat_axis=0, tiled=True)
    channel_count = lax.axis_size("gz") * mixed_sum.shape[0]
    sum_terms = lax.psum(jnp.sum(mixed_sum, axis=0), "gz")
    mix_average = sum_terms / channel_count
    mix_centered = mixed_sum - mix_average
    mix_spread = lax.psum(jnp.sum(jnp.square(mix_centered), axis=0), "gz") / channel_count
    local_mix = (mix_centered * lax.rsqrt(mix_spread + epsilon) * out_gain[:, None, None]).astype(
        jnp.bfloat16
    )
    normed_mix = lax.all_gather(local_mix, "gz", axis=0, tiled=True)
    projected = jnp.einsum("hij,hd->dij", normed_mix, w_out, preferred_element_type=jnp.float32)
    return (out_gate * projected).astype(jnp.bfloat16)


def solution(mesh):
    placed = (
        P("gz", "gy", "gx"),
        P("gy", "gx"),
        P(),
        P(None, "gz"),
        P(None, "gz"),
        P(None, "gz"),
        P(None, "gz"),
        P(None, "gz"),
        P("gz"),
        P(None, "gz"),
    )
    return jax.shard_map(
        local, mesh=mesh, in_specs=placed, out_specs=P("gz", "gy", "gx"), check_vma=False
    )
```

profile of v0, /device:TPU:0, one launch (start us, length us, event | category | flops | bytes accessed | tf_op | source)
XLA Modules:
  0.0 1984.1 jit_solution(8913950968688597543)
XLA Ops:
  6.5 0.0 copy-start
  6.5 0.0 all-gather.4.cloned.1.call-start
  6.5 0.7 all-gather.4.cloned.1.call-update
  7.3 0.0 all-gather.6.cloned.1.call-start
  7.3 1.1 convert_element_type.23
  8.4 564.6 %all-gather.4.cloned.1.call-done = bf16[128,512,256]{2,1,0:T(8,128)(2,1)} async-done(((bf16[32,512,256]{2,1,0:T(8,128)(2,1)}), bf16[128,512,256]{2,1,0:T(8,128)(2,1)}) %all-gather.4.cloned.1.call-update) | async-done | bytes 33554448 | tf_op jit(solution)/shard_map/all_gather | solution.py:21
  573.0 11.4 convert_reduce_fusion
  584.5 0.0 copy-start.4
  584.5 11.7 fusion.2
  596.2 0.1 add_rsqrt_fusion.1
  596.2 0.0 copy-done.4
  596.2 23.0 %fusion.4 = bf16[128,512,256]{2,1,0:T(8,128)(2,1)} fusion(bf16[128,512,256]{2,1,0:T(8,128)(2,1)} %all-gather.4.cloned.1.call-done, f32[128]{0:T(128)S(1)} %copy-done.4, f32[512,256]{1,0:T(8,128)S(1)} %add_rsqrt_fusion.1, f32[512,256]{1,0:T(8,128)S(1)} %broadcast_multiply_fusion.1), kind=kLoop, calls=%fused_computation.6 | loop fusion | flops 83886080 | bytes 68157952 | tf_op jit(solution)/shard_map/convert_element_type | solution.py:25
  619.3 0.0 copy-done
  619.3 0.0 copy-start.6
  619.3 35.7 %fusion.11 = f32[512,256,32]{1,2,0:T(8,128)} fusion(bf16[128,512,256]{2,1,0:T(8,128)(2,1)} %fusion.4, bf16[128,32]{0,1:T(8,128)(2,1)S(1)} %copy-done), kind=kOutput, calls=%fused_computation.13 | convolution fusion | flops 1073741824 | bytes 50339840 | tf_op jit(solution)/shard_map/cik,ch->hik/dot_general | solution.py:29
  655.0 0.0 copy-done.6
  655.0 38.1 %fusion.28 = bf16[32,512,256]{2,0,1:T(8,128)(2,1)} fusion(bf16[128,512,256]{2,1,0:T(8,128)(2,1)} %fusion.4, f32[512,256,32]{1,2,0:T(8,128)} %fusion.11, f32[512,256]{1,0:T(8,128)S(1)} %convert_element_type.23, bf16[128,32]{0,1:T(8,128)(2,1)S(1)} %copy-done.6), kind=kOutput, calls=%fused_computation.32 | convolution fusion | flops 1098907648 | bytes 59252736 | tf_op jit(solution)/shard_map/cik,ch->hik/dot_general | solution.py:29
  693.1 11.4 copy.27
  704.5 97.4 %all_to_all.54 = bf16[32,512,256]{2,1,0:T(8,128)(2,1)S(1)} all-to-all(bf16[32,512,256]{2,1,0:T(8,128)(2,1)} %copy.27), channel_id=1, replica_groups=mesh['gx'=4,'gy'=2,'gz'=4] {'gx'}, dimensions={0} | all-to-all | bytes 16777216 | tf_op jit(solution)/shard_map/all_to_all | solution.py:42
  801.8 7.3 copy.52
  809.1 0.0 copy-start.2
  809.1 14.3 all_to_all.46
  823.5 0.0 all-gather.6.cloned.1.call-update
  823.5 0.0 copy-start.7
  823.5 0.0 all-reduce.3.cloned.1.call-start
  823.5 0.0 copy-done.2
  823.5 37.6 %fusion.7 = f32[512,256,32]{1,2,0:T(8,128)} fusion(bf16[128,512,256]{2,1,0:T(8,128)(2,1)} %fusion.4, bf16[128,32]{0,1:T(8,128)(2,1)S(1)} %copy-done.2), kind=kOutput, calls=%fused_computation.9 | convolution fusion | flops 1073741824 | bytes 50339840 | tf_op jit(solution)/shard_map/cik,ch->hik/dot_general | solution.py:29
  861.2 0.0 copy-done.7
  861.2 38.1 %fusion.25 = bf16[32,512,256]{2,0,1:T(8,128)(2,1)} fusion(bf16[128,512,256]{2,1,0:T(8,128)(2,1)} %fusion.4, f32[512,256,32]{1,2,0:T(8,128)} %fusion.7, f32[512,256]{1,0:T(8,128)S(1)} %convert_element_type.23, bf16[128,32]{0,1:T(8,128)(2,1)S(1)} %copy-done.7), kind=kOutput, calls=%fused_computation.31 | convolution fusion | flops 1098907648 | bytes 59252736 | tf_op jit(solution)/shard_map/cik,ch->hik/dot_general | solution.py:29
  899.3 11.4 copy.23
  910.7 94.8 %all_to_all.55 = bf16[32,512,256]{2,1,0:T(8,128)(2,1)S(1)} all-to-all(bf16[32,512,256]{2,1,0:T(8,128)(2,1)} %copy.23), channel_id=1, replica_groups=mesh['gx'=4,'gy'=2,'gz'=4] {'gx'}, dimensions={0} | all-to-all | bytes 16777216 | tf_op jit(solution)/shard_map/all_to_all | solution.py:41
  1005.5 7.3 copy.53
  1012.8 14.3 all_to_all.42
  1027.1 0.0 all-gather.6.cloned.1.call-done
  1027.1 17.0 fusion.37
  1044.0 17.6 copy.29
  1061.6 190.6 %all_to_all.56 = f32[8,512,1024]{1,0,2:T(8,128)} all-to-all(f32[8,512,1024]{1,0,2:T(8,128)} %copy.29), channel_id=1, replica_groups=mesh['gx'=4,'gy'=2,'gz'=4] {'gx'}, dimensions={2} | all-to-all | bytes 33554432 | tf_op jit(solution)/shard_map/all_to_all | solution.py:50
  1252.3 20.2 %copy.30 = f32[8,512,4,256]{3,0,2,1:T(8,128)} copy(f32[8,512,4,256]{1,0,3,2:T(8,128)} %bitcast.52) | data formatting | bytes 33554432 | tf_op jit(solution)/shard_map/all_to_all | solution.py:50
  1272.5 0.0 copy-start.5
  1272.5 9.5 bitcast_reduce_fusion
  1282.0 0.0 all-reduce.3.cloned.1.call-update
  1282.0 0.0 all-reduce.5.cloned.1.call-start
  1282.1 36.2 %all-reduce.3.cloned.1.call-done = f32[512,256]{1,0:T(8,128)} async-done(((f32[512,256]{1,0:T(8,128)}), f32[512,256]{1,0:T(8,128)}) %all-reduce.3.cloned.1.call-update) | async-done | bytes 524304 | tf_op jit(solution)/shard_map/psum | solution.py:52
  1318.2 1.1 broadcast_multiply_fusion
  1319.3 12.2 fusion.19
  1331.5 0.0 all-reduce.5.cloned.1.call-update
  1331.5 0.0 all-gather.8.cloned.1.call-start
  1331.6 38.6 %all-reduce.5.cloned.1.call-done = f32[512,256]{1,0:T(8,128)} async-done(((f32[512,256]{1,0:T(8,128)}), f32[512,256]{1,0:T(8,128)}) %all-reduce.5.cloned.1.call-update) | async-done | bytes 524304 | tf_op jit(solution)/shard_map/psum | solution.py:55
  1370.1 1.1 add_rsqrt_fusion
  1371.2 0.0 copy-done.5
  1371.3 0.0 copy-start.3
  1371.3 11.1 fusion.17
  1382.4 0.0 all-gather.8.cloned.1.call-update
  1382.4 0.0 copy-done.3
  1382.4 0.0 copy-start.8
  1382.4 35.8 %fusion.5 = f32[512,256,32]{1,2,0:T(8,128)} fusion(bf16[128,512,256]{2,1,0:T(8,128)(2,1)} %fusion.4, bf16[128,32]{0,1:T(8,128)(2,1)S(1)} %copy-done.3), kind=kOutput, calls=%fused_computation.7 | convolution fusion | flops 1073741824 | bytes 50339840 | tf_op jit(solution)/shard_map/cij,cd->dij/dot_general | solution.py:38
  1418.2 525.5 %all-gather.8.cloned.1.call-done = bf16[128,512,256]{2,0,1:T(8,128)(2,1)} async-done(((bf16[32,512,256]{2,0,1:T(8,128)(2,1)}), bf16[128,512,256]{2,0,1:T(8,128)(2,1)}) %all-gather.8.cloned.1.call-update) | async-done | bytes 33554448 | tf_op jit(solution)/shard_map/all_gather | solution.py:59
  1943.7 0.0 copy-done.8
  1943.7 0.0 copy-start.1
  1943.8 21.8 %fusion.24 = bf16[32,512,256]{2,0,1:T(8,128)(2,1)} fusion(bf16[128,512,256]{2,0,1:T(8,128)(2,1)} %all-gather.8.cloned.1.call-done, f32[512,256,32]{1,2,0:T(8,128)} %fusion.5, bf16[128,32]{0,1:T(8,128)(2,1)S(1)} %copy-done.8), kind=kOutput, calls=%fused_computation.30 | convolution fusion | flops 1094713344 | bytes 58728448 | tf_op jit(solution)/shard_map/hij,hd->dij/dot_general | solution.py:60
  1965.6 11.5 copy.31
  1977.1 0.0 copy-done.1
  (1 shorter events, 0.0 us)
Async XLA Ops:
  6.5 612.8 %copy-start = (bf16[128,32]{0,1:T(8,128)(2,1)S(1)}, bf16[128,32]{0,1:T(8,128)(2,1)}, u32[]{:S(2)}) copy-start(bf16[128,32]{0,1:T(8,128)(2,1)} %param.16) | copy-start | bytes 24580
  6.5 566.5 %all-gather.4.cloned.1.call-start = ((), (), s32[]{:S(2)}) async-start(), calls=%async_computation.3 | async-start | bytes 41943040 | tf_op jit(solution)/shard_map/all_gather | solution.py:21
  7.3 1019.8 %all-gather.6.cloned.1.call-start = ((), (), s32[]{:S(2)}) async-start(), calls=%async_computation.4 | async-start | bytes 25165824 | tf_op jit(solution)/shard_map/all_gather | solution.py:46
  584.5 11.8 copy-start.4
  619.3 35.7 %copy-start.6 = (bf16[128,32]{0,1:T(8,128)(2,1)S(1)}, bf16[128,32]{0,1:T(8,128)(2,1)}, u32[]{:S(2)}) copy-start(bf16[128,32]{0,1:T(8,128)(2,1)} %param.15) | copy-start | bytes 24580
  809.1 14.4 copy-start.2
  823.5 37.7 %copy-start.7 = (bf16[128,32]{0,1:T(8,128)(2,1)S(1)}, bf16[128,32]{0,1:T(8,128)(2,1)}, u32[]{:S(2)}) copy-start(bf16[128,32]{0,1:T(8,128)(2,1)} %param.13) | copy-start | bytes 24580
  823.5 494.7 %all-reduce.3.cloned.1.call-start = ((), (), s32[]{:S(2)}) async-start(), calls=%async_computation.5 | async-start | bytes 1048576 | tf_op jit(solution)/shard_map/psum | solution.py:52
  1272.5 98.7 %copy-start.5 = (f32[32]{0:T(128)S(1)}, f32[32]{0:T(128)}, u32[]{:S(2)}) copy-start(f32[32]{0:T(128)} %param.18) | copy-start | bytes 388
  1282.0 88.1 %all-reduce.5.cloned.1.call-start = ((), (), s32[]{:S(2)}) async-start(), calls=%async_computation.6 | async-start | bytes 1048576 | tf_op jit(solution)/shard_map/psum | solution.py:55
  1331.5 612.2 %all-gather.8.cloned.1.call-start = ((), (), s32[]{:S(2)}) async-start(), calls=%async_computation.7 | async-start | bytes 41943040 | tf_op jit(solution)/shard_map/all_gather | solution.py:59
  1371.3 11.1 copy-start.3
  1382.4 561.3 %copy-start.8 = (bf16[128,32]{0,1:T(8,128)(2,1)S(1)}, bf16[128,32]{0,1:T(8,128)(2,1)}, u32[]{:S(2)}) copy-start(bf16[128,32]{0,1:T(8,128)(2,1)} %param.19) | copy-start | bytes 24580
  1943.7 33.4 %copy-start.1 = (bf16[128,32]{0,1:T(8,128)(2,1)S(1)}, bf16[128,32]{0,1:T(8,128)(2,1)}, u32[]{:S(2)}) copy-start(bf16[128,32]{0,1:T(8,128)(2,1)} %param.16) | copy-start | bytes 24580
Sparse Core Ops, SparseCore 0:
  8.9 564.0 all-gather.3
  823.6 26.7 all-gather.5
  1282.1 36.0 all-reduce.2
  1331.6 38.4 all-reduce.4
  1382.5 561.1 all-gather.7
where the time goes:
time: 1990 us; the launch traced here: 1980 us
  waiting for transfers between devices  1170 us (59%)
  blocking collectives  383 us (19%)
  matrix products  224 us (11%)
  local copies, waits for them, and re-layouts  115 us (6%)
  other arithmetic  82.3 us (4%)
    all_gather x1, waiting for transfers between devices, local(): lax.all_gather(pair, 'gz', axis=0, tiled=True).astype(jnp.float32)  565 us
    all_gather x1, waiting for transfers between devices, local(): normed_mix = lax.all_gather(local_mix, 'gz', axis=0, tiled=True)  526 us
    all_to_all x1, blocking collectives, local(): lax.all_to_all(full_product, 'gx', split_axis=2, concat_axis=0, tiled=True)  191 us
    dot_general x4, matrix products, project(): jnp.einsum('cik,ch->hik', normed, weight, preferred_element_type=jnp.floa...  150 us
    all_to_all x1, blocking collectives, local(): lax.all_to_all(right_rows, 'gx', split_axis=0, concat_axis=2, tiled=True)  97.4 us
    all_to_all x1, blocking collectives, local(): lax.all_to_all(left_rows, 'gx', split_axis=0, concat_axis=2, tiled=True)  94.8 us
  transfers between devices with their start and end apart: 5, of which 4 were waited for; matrix products, arithmetic and copies ran while one was open for 7% of the time, Pallas kernels for 0%

commit v1 on v0

--- a/solution.py
+++ b/solution.py
@@ -47,7 +47,10 @@
         (((2,), (2,)), ((0,), (0,))),
         preferred_element_type=jnp.float32,
     )
-    mixed_sum = lax.all_to_all(full_product, "gx", split_axis=2, concat_axis=0, tiled=True)
+    mixed_sum = jnp.concatenate(
+        lax.all_to_all(jnp.stack(jnp.split(full_product, lax.axis_size("gx"), axis=2)), "gx", 0, 0),
+        axis=0,
+    )
     channel_count = lax.axis_size("gz") * mixed_sum.shape[0]
     sum_terms = lax.psum(jnp.sum(mixed_sum, axis=0), "gz")
     mix_average = sum_terms / channel_count

time: 1990 us -> 1960 us (0.985)
  local copies, waits for them, and re-layouts: 115 us -> 84.3 us
    all_to_all x1 -> x0, local copies, waits for them, and re-layouts: 20.2 us -> none  [local(): lax.all_to_all(full_product, 'gx', split_axis=2, concat_axis=0, tiled=True)]
where the time goes in v1:
time: 1960 us; the launch traced here: 1950 us
  waiting for transfers between devices  1170 us (60%)
  blocking collectives  376 us (19%)
  matrix products  224 us (11%)
  local copies, waits for them, and re-layouts  84.3 us (4%)
  other arithmetic  84 us (4%)
    all_gather x1, waiting for transfers between devices, local(): lax.all_gather(pair, 'gz', axis=0, tiled=True).astype(jnp.float32)  565 us
    all_gather x1, waiting for transfers between devices, local(): normed_mix = lax.all_gather(local_mix, 'gz', axis=0, tiled=True)  525 us
    all_to_all x1, blocking collectives, local(): lax.all_to_all(jnp.stack(jnp.split(full_product, lax.axis_size('gx'), axi...  184 us
    dot_general x4, matrix products, project(): jnp.einsum('cik,ch->hik', normed, weight, preferred_element_type=jnp.floa...  149 us
    all_to_all x1, blocking collectives, local(): lax.all_to_all(right_rows, 'gx', split_axis=0, concat_axis=2, tiled=True)  97.4 us
    all_to_all x1, blocking collectives, local(): lax.all_to_all(left_rows, 'gx', split_axis=0, concat_axis=2, tiled=True)  94.8 us
  transfers between devices with their start and end apart: 5, of which 4 were waited for; matrix products, arithmetic and copies ran while one was open for 7% of the time, Pallas kernels for 0%

profile of v1, /device:TPU:0, one launch (start us, length us, event | category | flops | bytes accessed | tf_op | source)
XLA Modules:
  0.0 1947.9 jit_solution(2516835165825366884)
XLA Ops:
  6.5 0.0 copy-start
  6.5 0.0 all-gather.4.cloned.1.call-start
  6.5 0.7 all-gather.4.cloned.1.call-update
  7.3 0.0 all-gather.6.cloned.1.call-start
  7.3 1.1 convert_element_type.23
  8.4 564.6 %all-gather.4.cloned.1.call-done = bf16[128,512,256]{2,1,0:T(8,128)(2,1)} async-done(((bf16[32,512,256]{2,1,0:T(8,128)(2,1)}), bf16[128,512,256]{2,1,0:T(8,128)(2,1)}) %all-gather.4.cloned.1.call-update) | async-done | bytes 33554448 | tf_op jit(solution)/shard_map/all_gather | solution.py:21
  573.0 11.4 convert_reduce_fusion
  584.5 0.0 copy-start.4
  584.5 11.7 fusion.2
  596.2 0.1 add_rsqrt_fusion.1
  596.2 0.0 copy-done.4
  596.2 23.0 %fusion.4 = bf16[128,512,256]{2,1,0:T(8,128)(2,1)} fusion(bf16[128,512,256]{2,1,0:T(8,128)(2,1)} %all-gather.4.cloned.1.call-done, f32[128]{0:T(128)S(1)} %copy-done.4, f32[512,256]{1,0:T(8,128)S(1)} %add_rsqrt_fusion.1, f32[512,256]{1,0:T(8,128)S(1)} %broadcast_multiply_fusion.1), kind=kLoop, calls=%fused_computation.6 | loop fusion | flops 83886080 | bytes 68157952 | tf_op jit(solution)/shard_map/convert_element_type | solution.py:25
  619.2 0.0 copy-done
  619.2 0.0 copy-start.6
  619.2 35.7 %fusion.11 = f32[512,256,32]{1,2,0:T(8,128)} fusion(bf16[128,512,256]{2,1,0:T(8,128)(2,1)} %fusion.4, bf16[128,32]{0,1:T(8,128)(2,1)S(1)} %copy-done), kind=kOutput, calls=%fused_computation.13 | convolution fusion | flops 1073741824 | bytes 50339840 | tf_op jit(solution)/shard_map/cik,ch->hik/dot_general | solution.py:29
  654.9 0.0 copy-done.6
  654.9 38.1 %fusion.26 = bf16[32,512,256]{2,0,1:T(8,128)(2,1)} fusion(bf16[128,512,256]{2,1,0:T(8,128)(2,1)} %fusion.4, f32[512,256,32]{1,2,0:T(8,128)} %fusion.11, f32[512,256]{1,0:T(8,128)S(1)} %convert_element_type.23, bf16[128,32]{0,1:T(8,128)(2,1)S(1)} %copy-done.6), kind=kOutput, calls=%fused_computation.30 | convolution fusion | flops 1098907648 | bytes 59252736 | tf_op jit(solution)/shard_map/cik,ch->hik/dot_general | solution.py:29
  693.0 11.4 copy.27
  704.4 97.4 %all_to_all.41 = bf16[32,512,256]{2,1,0:T(8,128)(2,1)S(1)} all-to-all(bf16[32,512,256]{2,1,0:T(8,128)(2,1)} %copy.27), channel_id=1, replica_groups=mesh['gx'=4,'gy'=2,'gz'=4] {'gx'}, dimensions={0} | all-to-all | bytes 16777216 | tf_op jit(solution)/shard_map/all_to_all | solution.py:42
  801.7 7.3 copy.58
  809.0 0.0 copy-start.2
  809.0 14.3 all_to_all.36
  823.3 0.0 all-gather.6.cloned.1.call-update
  823.4 0.0 copy-start.7
  823.4 0.0 all-reduce.3.cloned.1.call-start
  823.4 0.0 copy-done.2
  823.4 37.6 %fusion.7 = f32[512,256,32]{1,2,0:T(8,128)} fusion(bf16[128,512,256]{2,1,0:T(8,128)(2,1)} %fusion.4, bf16[128,32]{0,1:T(8,128)(2,1)S(1)} %copy-done.2), kind=kOutput, calls=%fused_computation.9 | convolution fusion | flops 1073741824 | bytes 50339840 | tf_op jit(solution)/shard_map/cik,ch->hik/dot_general | solution.py:29
  861.0 0.0 copy-done.7
  861.0 38.1 %fusion.23 = bf16[32,512,256]{2,0,1:T(8,128)(2,1)} fusion(bf16[128,512,256]{2,1,0:T(8,128)(2,1)} %fusion.4, f32[512,256,32]{1,2,0:T(8,128)} %fusion.7, f32[512,256]{1,0:T(8,128)S(1)} %convert_element_type.23, bf16[128,32]{0,1:T(8,128)(2,1)S(1)} %copy-done.7), kind=kOutput, calls=%fused_computation.29 | convolution fusion | flops 1098907648 | bytes 59252736 | tf_op jit(solution)/shard_map/cik,ch->hik/dot_general | solution.py:29
  899.2 11.4 copy.23
  910.5 94.8 %all_to_all.42 = bf16[32,512,256]{2,1,0:T(8,128)(2,1)S(1)} all-to-all(bf16[32,512,256]{2,1,0:T(8,128)(2,1)} %copy.23), channel_id=1, replica_groups=mesh['gx'=4,'gy'=2,'gz'=4] {'gx'}, dimensions={0} | all-to-all | bytes 16777216 | tf_op jit(solution)/shard_map/all_to_all | solution.py:41
  1005.4 7.3 copy.59
  1012.6 14.3 all_to_all.32
  1027.0 0.0 all-gather.6.cloned.1.call-done
  1027.0 17.0 fusion.35
  1043.9 6.7 slice_bitcast_fusion.3
  1050.7 1.3 pad_maximum_fusion
  1051.9 184.0 %all_to_all.43 = f32[4,8,512,256]{3,2,1,0:T(8,128)} all-to-all(f32[4,8,512,256]{3,2,1,0:T(8,128)S(1)} %pad_maximum_fusion), channel_id=1, replica_groups=mesh['gx'=4,'gy'=2,'gz'=4] {'gx'}, dimensions={0} | all-to-all | bytes 33554432 | tf_op jit(solution)/shard_map/all_to_all | solution.py:51
  1236.0 0.0 copy-start.5
  1236.0 7.7 reduce_sum.38
  1243.6 0.0 all-reduce.3.cloned.1.call-update
  1243.7 0.0 all-reduce.5.cloned.1.call-start
  1243.7 36.0 %all-reduce.3.cloned.1.call-done = f32[512,256]{1,0:T(8,128)} async-done(((f32[512,256]{1,0:T(8,128)}), f32[512,256]{1,0:T(8,128)}) %all-reduce.3.cloned.1.call-update) | async-done | bytes 524304 | tf_op jit(solution)/shard_map/psum | solution.py:55
  1279.7 1.1 broadcast_multiply_fusion
  1280.8 8.5 multiply_reduce_fusion
  1289.3 0.0 all-reduce.5.cloned.1.call-update
  1289.3 0.0 all-gather.8.cloned.1.call-start
  1289.4 38.6 %all-reduce.5.cloned.1.call-done = f32[512,256]{1,0:T(8,128)} async-done(((f32[512,256]{1,0:T(8,128)}), f32[512,256]{1,0:T(8,128)}) %all-reduce.5.cloned.1.call-update) | async-done | bytes 524304 | tf_op jit(solution)/shard_map/psum | solution.py:58
  1327.9 1.1 add_rsqrt_fusion
  1329.1 0.0 copy-done.5
  1329.1 0.0 copy-start.3
  1329.1 17.1 fusion.17
  1346.2 0.0 all-gather.8.cloned.1.call-update
  1346.2 0.0 copy-done.3
  1346.2 0.0 copy-start.8
  1346.2 36.0 %fusion.5 = f32[512,256,32]{1,2,0:T(8,128)} fusion(bf16[128,512,256]{2,1,0:T(8,128)(2,1)} %fusion.4, bf16[128,32]{0,1:T(8,128)(2,1)S(1)} %copy-done.3), kind=kOutput, calls=%fused_computation.7 | convolution fusion | flops 1073741824 | bytes 50339840 | tf_op jit(solution)/shard_map/cij,cd->dij/dot_general | solution.py:38
  1382.2 525.3 %all-gather.8.cloned.1.call-done = bf16[128,512,256]{2,0,1:T(8,128)(2,1)} async-done(((bf16[32,512,256]{2,0,1:T(8,128)(2,1)}), bf16[128,512,256]{2,0,1:T(8,128)(2,1)}) %all-gather.8.cloned.1.call-update) | async-done | bytes 33554448 | tf_op jit(solution)/shard_map/all_gather | solution.py:62
  1907.5 0.0 copy-done.8
  1907.6 0.0 copy-start.1
  1907.6 21.8 %fusion.22 = bf16[32,512,256]{2,0,1:T(8,128)(2,1)} fusion(bf16[128,512,256]{2,0,1:T(8,128)(2,1)} %all-gather.8.cloned.1.call-done, f32[512,256,32]{1,2,0:T(8,128)} %fusion.5, bf16[128,32]{0,1:T(8,128)(2,1)S(1)} %copy-done.8), kind=kOutput, calls=%fused_computation.28 | convolution fusion | flops 1094713344 | bytes 58728448 | tf_op jit(solution)/shard_map/hij,hd->dij/dot_general | solution.py:63
  1929.4 11.5 copy.30
  1940.9 0.0 copy-done.1
  (1 shorter events, 0.0 us)
Async XLA Ops:
  6.5 612.7 %copy-start = (bf16[128,32]{0,1:T(8,128)(2,1)S(1)}, bf16[128,32]{0,1:T(8,128)(2,1)}, u32[]{:S(2)}) copy-start(bf16[128,32]{0,1:T(8,128)(2,1)} %param.16) | copy-start | bytes 24580
  6.5 566.5 %all-gather.4.cloned.1.call-start = ((), (), s32[]{:S(2)}) async-start(), calls=%async_computation.3 | async-start | bytes 41943040 | tf_op jit(solution)/shard_map/all_gather | solution.py:21
  7.3 1019.7 %all-gather.6.cloned.1.call-start = ((), (), s32[]{:S(2)}) async-start(), calls=%async_computation.4 | async-start | bytes 25165824 | tf_op jit(solution)/shard_map/all_gather | solution.py:46
  584.5 11.8 copy-start.4
  619.2 35.7 %copy-start.6 = (bf16[128,32]{0,1:T(8,128)(2,1)S(1)}, bf16[128,32]{0,1:T(8,128)(2,1)}, u32[]{:S(2)}) copy-start(bf16[128,32]{0,1:T(8,128)(2,1)} %param.15) | copy-start | bytes 24580
  809.0 14.4 copy-start.2
  823.4 37.7 %copy-start.7 = (bf16[128,32]{0,1:T(8,128)(2,1)S(1)}, bf16[128,32]{0,1:T(8,128)(2,1)}, u32[]{:S(2)}) copy-start(bf16[128,32]{0,1:T(8,128)(2,1)} %param.13) | copy-start | bytes 24580
  823.4 456.3 %all-reduce.3.cloned.1.call-start = ((), (), s32[]{:S(2)}) async-start(), calls=%async_computation.5 | async-start | bytes 1048576 | tf_op jit(solution)/shard_map/psum | solution.py:55
  1236.0 93.1 %copy-start.5 = (f32[32]{0:T(128)S(1)}, f32[32]{0:T(128)}, u32[]{:S(2)}) copy-start(f32[32]{0:T(128)} %param.18) | copy-start | bytes 388
  1243.7 84.3 %all-reduce.5.cloned.1.call-start = ((), (), s32[]{:S(2)}) async-start(), calls=%async_computation.6 | async-start | bytes 1048576 | tf_op jit(solution)/shard_map/psum | solution.py:58
  1289.3 618.2 %all-gather.8.cloned.1.call-start = ((), (), s32[]{:S(2)}) async-start(), calls=%async_computation.7 | async-start | bytes 41943040 | tf_op jit(solution)/shard_map/all_gather | solution.py:62
  1329.1 17.1 copy-start.3
  1346.2 561.3 %copy-start.8 = (bf16[128,32]{0,1:T(8,128)(2,1)S(1)}, bf16[128,32]{0,1:T(8,128)(2,1)}, u32[]{:S(2)}) copy-start(bf16[128,32]{0,1:T(8,128)(2,1)} %param.19) | copy-start | bytes 24580
  1907.6 33.4 %copy-start.1 = (bf16[128,32]{0,1:T(8,128)(2,1)S(1)}, bf16[128,32]{0,1:T(8,128)(2,1)}, u32[]{:S(2)}) copy-start(bf16[128,32]{0,1:T(8,128)(2,1)} %param.16) | copy-start | bytes 24580
Sparse Core Ops, SparseCore 0:
  8.9 564.0 all-gather.3
  823.5 26.7 all-gather.5
  1243.8 35.8 all-reduce.2
  1289.4 38.4 all-reduce.4
  1346.3 561.1 all-gather.7
